TPU v7x, 32 devices: a whole 2x2x4 slice. The times are simulated.
32 devices in a mesh: section: 2 (over y), dp: 8 (over z, core), vocab: 2 (over x).
Axes of the slice: x: 2, y: 2, z: 4, core: 2. Of those that a mesh axis runs over, the one named last changes fastest.
Arguments:
- activations: bfloat16 [2, 1024, 2048], P('section', 'dp'), may hold values from -32 to 32
- token_ids: int32 [2, 1024], replicated, may hold values from 0 to 8191
- embed_table: bfloat16 [8192, 2048], P(('dp', 'vocab')), may hold values from -3 to 3
Outputs:
- tied_grad: bfloat16 [16, 2, 256, 2048], P(('dp', 'vocab'), 'section')
All inputs are finite; a program needn't handle non-finite values.
Results may differ from a plain program's by a relative error of at most 0.0029.
Values may be sent and summed in bfloat16 or wider, within the bound.
A program may use at most 128 MiB of HBM per device.

v0:
```python
import jax
import jax.numpy as jnp
from jax import lax
from jax.sharding import PartitionSpec as P


def from_partner(block, axis, apart):
    count = lax.axis_size(axis)
    route = []
    for low in range(count):
        high = low | 1 << apart
        if high != low and high < count:
            route += [(low, high), (high, low)]
    return lax.ppermute(block, axis, route)


def spread_rows(row_tuple):
    return (
        lax.all_gather(row_tuple[0], "dp", axis=0, tiled=True),
        lax.all_gather(row_tuple[1], "dp", axis=0, tiled=True),
    )


def local_stats(logits):
    row_peak = jnp.max(logits, axis=1)
    row_total = jnp.sum(jnp.exp(logits - row_peak[:, None]), axis=1)
    return (row_peak, row_total)


def body(activations, token_ids, embed_table):
    own_rows = activations[0]
    model_width = own_rows.shape[1]
    table_count = embed_table.shape[0]
    section_index = lax.axis_index("section")
    half_rows = table_count // lax.axis_size("section")
    block_first = (
        lax.axis_index("dp") * lax.axis_size("vocab") + lax.axis_index("vocab")
    ) * table_count
    partner = from_partner(own_rows, "section", 0)
    cot_rows = jnp.where(section_index == 0, own_rows, partner)
    hid_rows = jnp.where(section_index == 0, partner, own_rows)
    cot_all, hid_all = spread_rows((cot_rows, hid_rows))
    my_table = lax.dynamic_slice_in_dim(embed_table, section_index * half_rows, half_rows, 0)
    row_first = block_first + section_index * half_rows
    positions = jnp.arange(half_rows, dtype=jnp.int32)[None, :]
    target_hot = (token_ids[1] - row_first)[:, None] == positions
    input_hot = (token_ids[0] - row_first)[:, None] == positions
    logits = lax.dot_general(
        hid_all, my_table, (((1,), (1,)), ((), ())), preferred_element_type=jnp.float32
    )
    row_peak, row_total = local_stats(logits)
    peak_all = lax.pmax(row_peak, ("section", "dp", "vocab"))
    total_all = lax.psum(row_total * jnp.exp(row_peak - peak_all), ("section", "dp", "vocab"))
    probs = jnp.exp(logits - peak_all[:, None]) / total_all[:, None]
    last_part = (probs - target_hot.astype(jnp.float32)).astype(jnp.bfloat16)
    first_part = input_hot.astype(jnp.bfloat16)
    summed = lax.dot_general(
        last_part, hid_all, (((0,), (0,)), ((), ())), preferred_element_type=jnp.float32
    )
    summed = summed + lax.dot_general(
        first_part, cot_all, (((0,), (0,)), ((), ())), preferred_element_type=jnp.float32
    )
    return summed.astype(jnp.bfloat16).reshape(1, 1, half_rows, model_width)


def solution(mesh):
    return jax.shard_map(
        body,
        mesh=mesh,
        in_specs=(P("section", "dp", None), P(), P(("dp", "vocab"), None)),
        out_specs=P(("dp", "vocab"), "section", None, None),
        check_vma=False,
    )
```

profile of v0, /device:TPU:0, one launch (start us, length us, event | category | flops | bytes accessed | tf_op | source)
XLA Modules:
  0.0 170.4 jit_solution(3358210218269821049)
XLA Ops:
  6.5 0.0 copy-start
  6.5 0.0 all-gather.3.cloned.1.call-start
  6.5 3.0 %collective-permute-start = (bf16[128,2048]{1,0:T(8,128)(2,1)}, bf16[128,2048]{1,0:T(8,128)(2,1)S(1)}, u32[]{:S(2)}, u32[]{:S(2)}) collective-permute-start(bf16[128,2048]{1,0:T(8,128)(2,1)} %bitcast.10), channel_id=1, source_target_pairs={{0,16},{16,0},{1,17},{17,1},{2,18},{18,2},{3,19},{19,3},{4,20},{20... | collective-permute-start | bytes 1572872 | tf_op jit(solution)/shard_map/ppermute | solution.py:14
  9.5 12.1 %collective-permute-done = bf16[128,2048]{1,0:T(8,128)(2,1)S(1)} collective-permute-done((bf16[128,2048]{1,0:T(8,128)(2,1)}, bf16[128,2048]{1,0:T(8,128)(2,1)S(1)}, u32[]{:S(2)}, u32[]{:S(2)}) %collective-permute-start) | collective-permute-done | bytes 524320 | tf_op jit(solution)/shard_map/ppermute | solution.py:14
  21.7 2.1 %broadcast_select_fusion.1 = (bf16[128,2048]{1,0:T(8,128)(2,1)}, bf16[128,2048]{1,0:T(8,128)(2,1)}) fusion(bf16[128,2048]{1,0:T(8,128)(2,1)S(1)} %collective-permute-done, pred[]{:T(512)S(6)} %eq.14, bf16[1,128,2048]{2,1,0:T(8,128)(2,1)} %param.3), kind=kLoop, calls=%fused_computation.15 | loop fusion | flops 524288 | bytes 2097153 | tf_op jit(solution)/shard_map/jit(_where)/select_n | solution.py:41
  23.8 0.0 all-gather.3.cloned.1.call-update
  23.8 0.0 all-gather.5.cloned.1.call-start
  23.9 0.7 all-gather.5.cloned.1.call-update
  24.6 0.8 slice_subtract_fusion.1
  25.4 46.9 %all-gather.3.cloned.1.call-done = bf16[1024,2048]{1,0:T(8,128)(2,1)} async-done(((bf16[128,2048]{1,0:T(8,128)(2,1)}), bf16[1024,2048]{1,0:T(8,128)(2,1)}) %all-gather.3.cloned.1.call-update) | async-done | bytes 4194320 | tf_op jit(solution)/shard_map/all_gather | solution.py:20
  72.3 0.0 copy-done
  72.3 3.5 %fusion.10 = (f32[1024]{0:T(1024)S(1)}, f32[1024,256]{0,1:T(8,128)S(1)}) fusion(bf16[1024,2048]{1,0:T(8,128)(2,1)} %all-gather.3.cloned.1.call-done, bf16[512,2048]{1,0:T(8,128)(2,1)S(1)} %copy-done, s32[]{:T(128)S(6)} %select_n.17), kind=kOutput, calls=%fused_computation.20 | convolution fusion | flops 1074002944 | bytes 6295556 | tf_op jit(solution)/shard_map/dot_general | solution.py:48
  75.8 42.2 %pmax.7 = f32[1024]{0:T(1024)S(1)} all-reduce(f32[1024]{0:T(1024)S(1)} %get-tuple-element.9), channel_id=1, replica_groups=mesh['section'=2,'dp'=8,'vocab'=2] {'section','dp','vocab'}, use_global_device_ids=true, to_apply=%region_1.2 | all-reduce | flops 1024 | bytes 8192 | tf_op jit(solution)/shard_map/pmax | solution.py:52
  118.0 0.2 exponential_reduce_fusion
  118.2 39.3 %psum.7 = f32[1024]{0:T(1024)S(1)} all-reduce(f32[1024]{0:T(1024)S(1)} %exponential_multiply_fusion), channel_id=1, replica_groups=mesh['section'=2,'dp'=8,'vocab'=2] {'section','dp','vocab'}, use_global_device_ids=true, to_apply=%region_3.4 | all-reduce | flops 1024 | bytes 8192 | tf_op jit(solution)/shard_map/psum | solution.py:53
  157.5 0.0 all-gather.5.cloned.1.call-done
  157.5 0.0 copy-start.1
  157.5 3.7 %fusion.4 = f32[256,2048]{1,0:T(8,128)S(1)} fusion(bf16[1024,2048]{1,0:T(8,128)(2,1)} %all-gather.5.cloned.1.call-done, s32[1024]{0:T(1024)S(1)} %bitcast.12), kind=kOutput, calls=%fused_computation.9 | convolution fusion | flops 1074003968 | bytes 6295552 | tf_op jit(solution)/shard_map/dot_general | solution.py:60
  161.2 0.0 copy-done.1
  161.2 2.3 %fusion.1 = bf16[1,1,256,2048]{3,2,1,0:T(8,128)(2,1)} fusion(f32[256,2048]{1,0:T(8,128)S(1)} %fusion.4, bf16[1024,2048]{1,0:T(8,128)(2,1)S(1)} %copy-done.1, f32[1024,256]{0,1:T(8,128)S(1)} %get-tuple-element.10, s32[1024]{0:T(1024)S(1)} %bitcast.11, f32[1024]{0:T(1024)S(1)} %psum.7, f32[1024]{0:T(1024)S(1)} %pmax.7), kind=kOutput, calls=%fused_computation.2 | convolution fusion | flops 1076363264 | bytes 8400896 | tf_op jit(solution)/shard_map/dot_general | solution.py:57
  (1 shorter events, 0.0 us)
Async XLA Ops:
  6.5 65.8 %copy-start = (bf16[512,2048]{1,0:T(8,128)(2,1)S(1)}, bf16[512,2048]{1,0:T(8,128)(2,1)}, u32[]{:S(2)}) copy-start(bf16[512,2048]{1,0:T(8,128)(2,1)} %param.5) | copy-start | bytes 6291460
  6.5 65.8 %all-gather.3.cloned.1.call-start = ((), (), s32[]{:S(2)}) async-start(), calls=%async_computation | async-start | bytes 4718592 | tf_op jit(solution)/shard_map/all_gather | solution.py:20
  6.5 15.1 %collective-permute-start = (bf16[128,2048]{1,0:T(8,128)(2,1)}, bf16[128,2048]{1,0:T(8,128)(2,1)S(1)}, u32[]{:S(2)}, u32[]{:S(2)}) collective-permute-start(bf16[128,2048]{1,0:T(8,128)(2,1)} %bitcast.10), channel_id=1, source_target_pairs={{0,16},{16,0},{1,17},{17,1},{2,18},{18,2},{3,19},{19,3},{4,20},{20... | collective-permute-start | bytes 1572872 | tf_op jit(solution)/shard_map/ppermute | solution.py:14
  23.8 133.7 %all-gather.5.cloned.1.call-start = ((), (), s32[]{:S(2)}) async-start(), calls=%async_computation.1 | async-start | bytes 4718592 | tf_op jit(solution)/shard_map/all_gather | solution.py:19
  157.5 3.7 %copy-start.1 = (bf16[1024,2048]{1,0:T(8,128)(2,1)S(1)}, bf16[1024,2048]{1,0:T(8,128)(2,1)}, u32[]{:S(2)}) copy-start(bf16[1024,2048]{1,0:T(8,128)(2,1)} %all-gather.3.cloned.1.call-done) | copy-start | bytes 12582916
Sparse Core Ops, SparseCore 0:
  23.9 48.3 all-gather.2
  73.9 46.7 all-gather.4
where the time goes:
time: 171 us; the launch traced here: 170 us
  blocking collectives  81.5 us (48%)
  waiting for transfers between devices  59.8 us (35%)
  between operations  13.4 us (8%)
  matrix products  9.52 us (6%)
  other arithmetic  3.09 us (2%)
  starting transfers between devices  3.04 us (2%)
    all_gather x1, waiting for transfers between devices, spread_rows(): lax.all_gather(row_tuple[1], 'dp', axis=0, tiled=True)  46.9 us
    pmax x1, blocking collectives, body(): peak_all = lax.pmax(row_peak, ('section', 'dp', 'vocab'))  42.2 us
    psum x1, blocking collectives, body(): lax.psum(row_total * jnp.exp(row_peak - peak_all), ('section', 'dp', 'voc...  39.3 us
    ppermute x1, waiting for transfers between devices, from_partner(): return lax.ppermute(block, axis, route)  12.1 us
    dot_general x1, matrix products, body(): lax.dot_general(first_part, cot_all, (((0,), (0,)), ((), ())), preferred_...  3.7 us
    dot_general x1, matrix products, body(): lax.dot_general(hid_all, my_table, (((1,), (1,)), ((), ())), preferred_el...  3.48 us
  transfers between devices with their start and end apart: 3, of which 2 were waited for; matrix products, arithmetic and copies ran while one was open for 3% of the time, Pallas kernels for 0%

commit v1 on v0

v1 whole, which is shorter than its diff:
```python
import functools

import jax
import jax.numpy as jnp
from jax import lax
from jax.experimental import pallas as pl
from jax.experimental.pallas import tpu as pltpu
from jax.sharding import PartitionSpec as P

MESH = pl.DeviceIdType.MESH
NT = (((1,), (1,)), ((), ()))


def kernel(sizes, ids_ref, act_ref, table_ref, out_ref, gathered, table, logits, col_stats,
           group_stats, chain_stats, load_sem, send_sem, recv_sem, stat_send, stat_recv,
           chain_send, chain_recv):
    n_dp, n_vocab, rows, tile = sizes
    n_z = n_dp // 2
    half = rows // 2
    s = lax.axis_index("section")
    d = lax.axis_index("dp")
    v = lax.axis_index("vocab")
    z = d // 2
    c = d % 2
    h = v % 2
    other = 1 - s
    pair = v + 1 - 2 * h
    table_rows = table.shape[0]
    half_rows = table_rows // 2
    targets = {
        "left": (s, d - 2, v),
        "right": (s, d + 2, v),
        "x": (s, d, pair),
        "y": (other, d, v),
        "sib": (s, d + 1 - 2 * c, v),
    }
    lane = {"left": 0, "right": 1, "x": 2, "y": 3, "sib": 4}

    own_load = pltpu.make_async_copy(
        act_ref.at[0], gathered.at[s, pl.ds(pl.multiple_of(d * rows, rows), rows)], load_sem.at[0]
    )
    own_load.start()
    table_load = pltpu.make_async_copy(table_ref, table, load_sem.at[1])
    table_load.start()

    barrier = pltpu.get_barrier_semaphore()

    def greet(sec, dp, voc):
        pl.semaphore_signal(barrier, inc=1, device_id=(sec, dp, voc), device_id_type=MESH)

    for sec in range(2):
        for core in range(2):
            for voc in range(n_vocab):
                is_me = (sec == s) & (core == c) & (voc == v)

                @pl.when(jnp.logical_not(is_me))
                def _():
                    greet(sec, z * 2 + core, voc)
        for zz in range(n_z):
            @pl.when(zz != z)
            def _():
                greet(sec, zz * 2 + c, v)
    pl.semaphore_wait(barrier, 4 * n_vocab - 1 + 2 * (n_z - 1))

    def piece(sec, dp, k):
        first = pl.multiple_of(dp * rows + k * half, half)
        return gathered.at[sec, pl.ds(first, half)]

    def copy(to, sec, dp, k):
        where = piece(sec, dp, k)
        return pltpu.make_async_remote_copy(
            src_ref=where, dst_ref=where,
            send_sem=send_sem.at[lane[to], sec, dp // 2, k],
            recv_sem=recv_sem.at[sec, dp, k],
            device_id=targets[to], device_id_type=MESH,
        )

    def need(to, own, zz, k):
        far = jnp.abs(zz - z) >= 2
        if to == "sib":
            return jnp.bool_(True)
        if own:
            if to == "right":
                return (zz <= z) & (z < n_z - 1) & ((zz == z) | (k == h))
            if to == "left":
                return (zz >= z) & (z > 0) & ((zz == z) | (k == h))
            if to == "x":
                return far & (k == h)
            return (zz == z) | (k == h)
        if to == "x":
            return (zz != z) & (k == h)
        return jnp.bool_(False)

    order_own = ("right", "left", "y", "x", "sib")
    order_other = ("x", "sib")

    def emit(own, zz, k):
        for to in order_own if own else order_other:
            @pl.when(need(to, own, zz, k))
            def _():
                copy(to, s if own else other, zz * 2 + c, k).start()

    def arrive(sec, dp, k):
        copy("sib", sec, dp, k).wait_recv()

    def score(dp):
        tokens = gathered.at[1, pl.ds(pl.multiple_of(dp * rows, rows), rows)]
        lanes = pl.ds(pl.multiple_of(dp * rows, rows), rows)

        @pl.when(s == 1)
        def _():
            scores = lax.dot_general(table[...], tokens[...], NT, preferred_element_type=jnp.float32)
            logits[:, lanes] = scores[half_rows:]
            peak = jnp.max(scores, axis=0, keepdims=True)
            total = jnp.sum(jnp.exp(scores - peak), axis=0, keepdims=True)
            col_stats[0:1, lanes] = peak
            col_stats[1:2, lanes] = total

        @pl.when(s == 0)
        def _():
            logits[:, lanes] = lax.dot_general(
                table[:half_rows], tokens[...], NT, preferred_element_type=jnp.float32
            )

    own_load.wait()
    emit(True, z, h)
    emit(True, z, 1 - h)
    table_load.wait()

    def others(delta, act):
        for zz in (z - delta, z + delta) if delta else (z,):
            @pl.when((zz >= 0) & (zz < n_z))
            def _():
                act(zz)

    def take(own, k_own):
        def act(zz):
            arrive(s if own else other, zz * 2 + c, k_own)
            emit(own, zz, k_own)
        return act

    for step in range(1, n_z + 2):
        if step < n_z:
            others(step, take(True, h))
        if step == 1:
            others(0, take(False, h))
            others(1, take(True, 1 - h))
            others(0, take(False, 1 - h))
        if 1 <= step - 1 < n_z:
            others(step - 1, take(False, h))
        if 2 <= step - 1 < n_z:
            others(step - 1, take(True, 1 - h))
        if 1 <= step - 2 < n_z:
            others(step - 2, take(False, 1 - h))

    def sibling(sec):
        def act(zz, carry):
            for k in range(2):
                arrive(sec, zz * 2 + 1 - c, k)
            return carry
        lax.fori_loop(0, n_z, act, 0)

    sibling(1)

    def score_all(dp, carry):
        score(dp)
        return carry

    lax.fori_loop(0, n_dp, score_all, 0)

    def combine(load, count):
        peak = load(0)[0:1]
        for i in range(1, count):
            peak = jnp.maximum(peak, load(i)[0:1])
        total = jnp.zeros_like(peak)
        for i in range(count):
            both = load(i)
            total = total + both[1:2] * jnp.exp(both[0:1] - peak)
        return peak, total

    n_group = 2 * n_vocab
    mine = c * n_vocab + v

    def group_copy(slot, target_core, target_voc):
        return pltpu.make_async_remote_copy(
            src_ref=group_stats.at[mine], dst_ref=group_stats.at[mine],
            send_sem=stat_send.at[slot], recv_sem=stat_recv.at[mine],
            device_id=(s, z * 2 + target_core, target_voc), device_id_type=MESH,
        )

    def chain_copy(sec, zz):
        return pltpu.make_async_remote_copy(
            src_ref=chain_stats.at[z], dst_ref=chain_stats.at[z],
            send_sem=chain_send.at[sec, zz], recv_sem=chain_recv.at[z],
            device_id=(sec, zz * 2 + c, v), device_id_type=MESH,
        )

    def landed(buffer, sems, slot):
        pltpu.make_async_copy(buffer.at[slot], buffer.at[slot], sems.at[slot]).wait()

    @pl.when(s == 1)
    def _():
        group_stats[mine] = col_stats[...]
        for slot in range(n_group):
            @pl.when(slot != mine)
            def _():
                group_copy(slot, slot // n_vocab, slot % n_vocab).start()
        for slot in range(n_group):
            @pl.when(slot != mine)
            def _():
                landed(group_stats, stat_recv, slot)
        peak, total = combine(lambda i: group_stats[i], n_group)
        chain_stats[z, 0:1] = peak
        chain_stats[z, 1:2] = total
        for zz in range(n_z):
            for sec in range(2):
                @pl.when((sec == 0) | (zz != z))
                def _():
                    chain_copy(sec, zz).start()
        for slot in range(n_group):
            @pl.when(slot != mine)
            def _():
                group_copy(slot, slot // n_vocab, slot % n_vocab).wait_send()

    for zz in range(n_z):
        @pl.when((s == 0) | (zz != z))
        def _():
            landed(chain_stats, chain_recv, zz)
    peak, total = combine(lambda i: chain_stats[i], n_z)

    first = (d * n_vocab + v) * table_rows + s * half_rows
    row = lax.broadcasted_iota(jnp.int32, logits.shape, 0) + first
    probs = jnp.exp(logits[...] - peak) * (1.0 / total)
    last = (probs - (ids_ref[1:2, :] == row).astype(jnp.float32)).astype(jnp.bfloat16)
    first_hot = (ids_ref[0:1, :] == row).astype(jnp.float32).astype(jnp.bfloat16)

    sibling(0)
    width = out_ref.shape[1]
    for at in range(0, width, tile):
        summed = jnp.dot(last, gathered[1, :, at:at + tile], preferred_element_type=jnp.float32)
        summed = summed + jnp.dot(
            first_hot, gathered[0, :, at:at + tile], preferred_element_type=jnp.float32
        )
        out_ref[:, at:at + tile] = summed.astype(jnp.bfloat16)

    @pl.when(s == 1)
    def _():
        for zz in range(n_z):
            for sec in range(2):
                @pl.when((sec == 0) | (zz != z))
                def _():
                    chain_copy(sec, zz).wait_send()

    def drain(zz, carry):
        for k in range(2):
            for own in (True, False):
                for to in order_own if own else order_other:
                    @pl.when(need(to, own, zz, k))
                    def _():
                        copy(to, s if own else other, zz * 2 + c, k).wait_send()
        return carry

    lax.fori_loop(0, n_z, drain, 0)


def solution(mesh):
    n_dp, n_vocab = mesh.shape["dp"], mesh.shape["vocab"]

    def body(activations, token_ids, embed_table):
        _, rows, width = activations.shape
        table_rows = embed_table.shape[0]
        tokens = rows * n_dp
        half_rows = table_rows // 2
        n_z = n_dp // 2
        dma = pltpu.SemaphoreType.DMA
        grad = pl.pallas_call(
            functools.partial(kernel, (n_dp, n_vocab, rows, min(512, width))),
            out_shape=jax.ShapeDtypeStruct((half_rows, width), jnp.bfloat16),
            in_specs=[
                pl.BlockSpec(memory_space=pltpu.VMEM),
                pl.BlockSpec(memory_space=pl.ANY),
                pl.BlockSpec(memory_space=pl.ANY),
            ],
            out_specs=pl.BlockSpec(memory_space=pltpu.VMEM),
            scratch_shapes=[
                pltpu.VMEM((2, tokens, width), jnp.bfloat16),
                pltpu.VMEM((table_rows, width), jnp.bfloat16),
                pltpu.VMEM((half_rows, tokens), jnp.float32),
                pltpu.VMEM((2, tokens), jnp.float32),
                pltpu.VMEM((2 * n_vocab, 2, tokens), jnp.float32),
                pltpu.VMEM((n_z, 2, tokens), jnp.float32),
                dma((2,)),
                dma((5, 2, n_z, 2)),
                dma((2, n_dp, 2)),
                dma((2 * n_vocab,)),
                dma((2 * n_vocab,)),
                dma((2, n_z)),
                dma((n_z,)),
            ],
            compiler_params=pltpu.CompilerParams(
                collective_id=0, has_side_effects=True, vmem_limit_bytes=60 * 1024 * 1024
            ),
        )(token_ids, activations, embed_table)
        return grad.reshape(1, 1, half_rows, width)

    return jax.shard_map(
        body,
        mesh=mesh,
        in_specs=(P("section", "dp", None), P(), P(("dp", "vocab"), None)),
        out_specs=P(("dp", "vocab"), "section", None, None),
        check_vma=False,
    )
```

time: 171 us -> 74.3 us (0.43)
  blocking collectives: 81.5 us -> 0 us
  Pallas kernels: 0 us -> 71.8 us
  waiting for transfers between devices: 59.8 us -> 0 us
  between operations: 13.4 us -> 0.01 us
  matrix products: 9.52 us -> 0 us
  other arithmetic: 3.09 us -> 0 us
  starting transfers between devices: 3.04 us -> 0 us
  local copies, waits for them, and re-layouts: 0.01 us -> 2.3 us
    pallas_call x0 -> x1, Pallas kernels: none -> 71.8 us  [body(): pl.pallas_call(functools.partial(kernel, (n_dp, n_vocab, rows, min(512, w...]
    all_gather x2 -> x0, waiting for transfers between devices: 46.9 us -> none  [the longest x1 46.9 us: spread_rows(): lax.all_gather(row_tuple[1], 'dp', axis=0, tiled=True)]
    pmax x1 -> x0, blocking collectives: 42.2 us -> none  [body(): peak_all = lax.pmax(row_peak, ('section', 'dp', 'vocab'))]
    psum x1 -> x0, blocking collectives: 39.3 us -> none  [body(): lax.psum(row_total * jnp.exp(row_peak - peak_all), ('section', 'dp', 'voc...]
    ppermute x1 -> x0, waiting for transfers between devices: 12.1 us -> none  [from_partner(): return lax.ppermute(block, axis, route)]
    dot_general x3 -> x0, matrix products: 9.52 us -> none  [the longest x1 3.7 us: body(): lax.dot_general(first_part, cot_all, (((0,), (0,)), ((), ())), preferred_...]
    ppermute x1 -> x0, starting transfers between devices: 3 us -> none  [from_partner(): return lax.ppermute(block, axis, route)]
    unnamed x4 -> x1, local copies, waits for them, and re-layouts: 0.01 us -> 2.3 us
  transfers between devices with their start and end apart: 3 -> 0, of which waited for: 2 -> 0; matrix products, arithmetic and copies ran while one was open for 3% -> 0% of each run, Pallas kernels for 0% -> 0%
where the time goes in v1:
time: 74.3 us; the launch traced here: 74.1 us
  Pallas kernels  71.8 us (97%)
  local copies, waits for them, and re-layouts  2.3 us (3%)
    pallas_call x1, Pallas kernels, body(): pl.pallas_call(functools.partial(kernel, (n_dp, n_vocab, rows, min(512, w...  71.8 us
    unnamed x1, local copies, waits for them, and re-layouts  2.3 us

profile of v1, /device:TPU:0, one launch (start us, length us, event | category | flops | bytes accessed | tf_op | source)
XLA Modules:
  0.0 74.1 jit_solution(2548349540898957235)
XLA Ops:
  0.0 71.8 %shard_map.37 = bf16[256,2048]{1,0:T(8,128)(2,1)} custom-call(s32[2,1024]{1,0:T(2,128)} %ids_ref.1, bf16[1,128,2048]{2,1,0:T(8,128)(2,1)} %act_ref.1, bf16[512,2048]{1,0:T(8,128)(2,1)} %table_ref.1), custom_call_target="tpu_custom_call" | custom-call | tf_op jit(solution)/shard_map/pallas_call | solution.py:276
  71.8 2.3 %copy.5 = bf16[1,1,256,2048]{3,2,1,0:T(8,128)(2,1)} copy(bf16[1,1,256,2048]{3,2,1,0:T(8,128)(2,1)} %bitcast.1) | data formatting | bytes 2097152

commit v2 on v1

--- a/solution.py
+++ b/solution.py
@@ -8,15 +8,17 @@
 from jax.sharding import PartitionSpec as P
 
 MESH = pl.DeviceIdType.MESH
+PARTS = 4
 NT = (((1,), (1,)), ((), ()))
 
 
 def kernel(sizes, ids_ref, act_ref, table_ref, out_ref, gathered, table, logits, col_stats,
            group_stats, chain_stats, load_sem, send_sem, recv_sem, stat_send, stat_recv,
            chain_send, chain_recv):
-    n_dp, n_vocab, rows, tile = sizes
+    n_dp, n_vocab, rows, parts, tile = sizes
     n_z = n_dp // 2
     half = rows // 2
+    part = half // parts
     s = lax.axis_index("section")
     d = lax.axis_index("dp")
     v = lax.axis_index("vocab")
@@ -62,21 +64,22 @@
                 greet(sec, zz * 2 + c, v)
     pl.semaphore_wait(barrier, 4 * n_vocab - 1 + 2 * (n_z - 1))
 
-    def piece(sec, dp, k):
-        first = pl.multiple_of(dp * rows + k * half, half)
-        return gathered.at[sec, pl.ds(first, half)]
-
-    def copy(to, sec, dp, k):
-        where = piece(sec, dp, k)
+    def piece(sec, dp, k, j):
+        first = pl.multiple_of(dp * rows + k * half + j * part, part)
+        return gathered.at[sec, pl.ds(first, part)]
+
+    def copy(to, sec, dp, k, j):
+        where = piece(sec, dp, k, j)
         return pltpu.make_async_remote_copy(
             src_ref=where, dst_ref=where,
-            send_sem=send_sem.at[lane[to], sec, dp // 2, k],
-            recv_sem=recv_sem.at[sec, dp, k],
+            send_sem=send_sem.at[lane[to], sec, dp // 2, k, j],
+            recv_sem=recv_sem.at[sec, dp, k, j],
             device_id=targets[to], device_id_type=MESH,
         )
 
+    twin = z + 1 - 2 * (z % 2)
+
     def need(to, own, zz, k):
-        far = jnp.abs(zz - z) >= 2
         if to == "sib":
             return jnp.bool_(True)
         if own:
@@ -85,23 +88,47 @@
             if to == "left":
                 return (zz >= z) & (z > 0) & ((zz == z) | (k == h))
             if to == "x":
-                return far & (k == h)
-            return (zz == z) | (k == h)
+                return (jnp.abs(zz - z) >= 2) & (k == h)
+            return (zz == twin) | (k == h)
         if to == "x":
-            return (zz != z) & (k == h)
+            return (zz != twin) & (k == h)
         return jnp.bool_(False)
 
     order_own = ("right", "left", "y", "x", "sib")
     order_other = ("x", "sib")
 
-    def emit(own, zz, k):
-        for to in order_own if own else order_other:
+    def emit(own, zz, k, j, lanes):
+        for to in lanes:
             @pl.when(need(to, own, zz, k))
             def _():
-                copy(to, s if own else other, zz * 2 + c, k).start()
-
-    def arrive(sec, dp, k):
-        copy("sib", sec, dp, k).wait_recv()
+                copy(to, s if own else other, zz * 2 + c, k, j).start()
+
+    def arrive(sec, dp, k, j):
+        copy("sib", sec, dp, k, j).wait_recv()
+
+    def event(own, zz, k, j):
+        arrive(s if own else other, zz * 2 + c, k, j)
+        emit(own, zz, k, j, order_own if own else order_other)
+
+    def each_part(act):
+        def one(j, carry):
+            act(j)
+            return carry
+        lax.fori_loop(0, parts, one, 0)
+
+    def from_y(index):
+        near = jnp.minimum(z, n_z - 1 - z)
+        paired = index < 2 * near * parts
+        inside = index % (2 * parts)
+        delta = index // (2 * parts) + 1
+        side = 2 * (inside % 2) - 1
+        rest = index - 2 * near * parts
+        far_side = jnp.where(z < n_z - 1 - z, 1, -1)
+        zz = jnp.where(paired, z + side * delta, z + far_side * (near + 1 + rest // parts))
+        return zz, jnp.where(paired, inside // 2, rest % parts)
+
+    def own_second_half(to):
+        each_part(lambda j: copy(to, s, d, 1 - h, j).start())
 
     def score(dp):
         tokens = gathered.at[1, pl.ds(pl.multiple_of(dp * rows, rows), rows)]
@@ -122,51 +149,71 @@
                 table[:half_rows], tokens[...], NT, preferred_element_type=jnp.float32
             )
 
-    own_load.wait()
-    emit(True, z, h)
-    emit(True, z, 1 - h)
-    table_load.wait()
-
-    def others(delta, act):
-        for zz in (z - delta, z + delta) if delta else (z,):
-            @pl.when((zz >= 0) & (zz < n_z))
-            def _():
-                act(zz)
-
-    def take(own, k_own):
-        def act(zz):
-            arrive(s if own else other, zz * 2 + c, k_own)
-            emit(own, zz, k_own)
-        return act
-
-    for step in range(1, n_z + 2):
-        if step < n_z:
-            others(step, take(True, h))
-        if step == 1:
-            others(0, take(False, h))
-            others(1, take(True, 1 - h))
-            others(0, take(False, 1 - h))
-        if 1 <= step - 1 < n_z:
-            others(step - 1, take(False, h))
-        if 2 <= step - 1 < n_z:
-            others(step - 1, take(True, 1 - h))
-        if 1 <= step - 2 < n_z:
-            others(step - 2, take(False, 1 - h))
+    def score_all():
+        def one(dp, carry):
+            score(dp)
+            return carry
+        lax.fori_loop(0, n_dp, one, 0)
 
     def sibling(sec):
         def act(zz, carry):
             for k in range(2):
-                arrive(sec, zz * 2 + 1 - c, k)
+                each_part(lambda j: arrive(sec, zz * 2 + 1 - c, k, j))
             return carry
         lax.fori_loop(0, n_z, act, 0)
 
-    sibling(1)
-
-    def score_all(dp, carry):
-        score(dp)
-        return carry
-
-    lax.fori_loop(0, n_dp, score_all, 0)
+    def on_both_sides(delta, act):
+        for zz in (z - delta, z + delta):
+            @pl.when((zz >= 0) & (zz < n_z))
+            def _():
+                act(zz)
+
+    own_load.wait()
+    each_part(lambda j: emit(True, z, h, j, ("right", "left", "y")))
+    each_part(lambda j: emit(True, z, h, j, ("sib",)))
+    each_part(lambda j: emit(True, z, 1 - h, j, ("sib",)))
+    pl.when((z > 0) & (z == n_z - 1))(lambda: own_second_half("left"))
+    pl.when((z == 0) & (z < n_z - 1))(lambda: own_second_half("right"))
+
+    def slot(t):
+        def links(j):
+            if t + 1 < n_z:
+                on_both_sides(t + 1, lambda zz: event(True, zz, h, j))
+            if t == 0:
+                event(False, z, h, j)
+            elif t < n_z:
+                zz, jj = from_y((t - 1) * parts + j)
+                event(False, zz, h, jj)
+
+        if t < n_z:
+            each_part(links)
+        if t < n_z - 1:
+            pl.when((z > 0) & (t == n_z - 2 - z))(lambda: own_second_half("left"))
+            pl.when((z < n_z - 1) & (t == z - 1))(lambda: own_second_half("right"))
+
+        def second(j):
+            if 1 <= t < n_z:
+                pl.when((z > 0) & (t == z))(lambda: event(True, z - 1, 1 - h, j))
+                pl.when((z < n_z - 1) & (t == n_z - 1 - z))(
+                    lambda: event(True, z + 1, 1 - h, j)
+                )
+            if t == 1:
+                event(False, z, 1 - h, j)
+            if 2 <= t < n_z:
+                on_both_sides(t, lambda zz: event(True, zz, 1 - h, j))
+            if t == n_z:
+                event(False, twin, 1 - h, j)
+            if 3 <= t:
+                zz, jj = from_y((t - 3) * parts + j)
+                pl.when(zz != twin)(lambda: event(False, zz, 1 - h, jj))
+
+        if t >= 1:
+            each_part(second)
+
+    for t in range(n_z):
+        slot(t)
+        if t == 0:
+            table_load.wait()
 
     def combine(load, count):
         peak = load(0)[0:1]
@@ -200,15 +247,22 @@
 
     @pl.when(s == 1)
     def _():
+        sibling(1)
+        score_all()
         group_stats[mine] = col_stats[...]
-        for slot in range(n_group):
-            @pl.when(slot != mine)
-            def _():
-                group_copy(slot, slot // n_vocab, slot % n_vocab).start()
-        for slot in range(n_group):
-            @pl.when(slot != mine)
-            def _():
-                landed(group_stats, stat_recv, slot)
+        for at in range(n_group):
+            @pl.when(at != mine)
+            def _():
+                group_copy(at, at // n_vocab, at % n_vocab).start()
+
+    slot(n_z)
+
+    @pl.when(s == 1)
+    def _():
+        for at in range(n_group):
+            @pl.when(at != mine)
+            def _():
+                landed(group_stats, stat_recv, at)
         peak, total = combine(lambda i: group_stats[i], n_group)
         chain_stats[z, 0:1] = peak
         chain_stats[z, 1:2] = total
@@ -217,10 +271,17 @@
                 @pl.when((sec == 0) | (zz != z))
                 def _():
                     chain_copy(sec, zz).start()
-        for slot in range(n_group):
-            @pl.when(slot != mine)
-            def _():
-                group_copy(slot, slot // n_vocab, slot % n_vocab).wait_send()
+        for at in range(n_group):
+            @pl.when(at != mine)
+            def _():
+                group_copy(at, at // n_vocab, at % n_vocab).wait_send()
+
+    slot(n_z + 1)
+
+    @pl.when(s == 0)
+    def _():
+        sibling(1)
+        score_all()
 
     for zz in range(n_z):
         @pl.when((s == 0) | (zz != z))
@@ -257,7 +318,8 @@
                 for to in order_own if own else order_other:
                     @pl.when(need(to, own, zz, k))
                     def _():
-                        copy(to, s if own else other, zz * 2 + c, k).wait_send()
+                        sec = s if own else other
+                        each_part(lambda j: copy(to, sec, zz * 2 + c, k, j).wait_send())
         return carry
 
     lax.fori_loop(0, n_z, drain, 0)
@@ -274,7 +336,7 @@
         n_z = n_dp // 2
         dma = pltpu.SemaphoreType.DMA
         grad = pl.pallas_call(
-            functools.partial(kernel, (n_dp, n_vocab, rows, min(512, width))),
+            functools.partial(kernel, (n_dp, n_vocab, rows, PARTS, min(512, width))),
             out_shape=jax.ShapeDtypeStruct((half_rows, width), jnp.bfloat16),
             in_specs=[
                 pl.BlockSpec(memory_space=pltpu.VMEM),
@@ -290,8 +352,8 @@
                 pltpu.VMEM((2 * n_vocab, 2, tokens), jnp.float32),
                 pltpu.VMEM((n_z, 2, tokens), jnp.float32),
                 dma((2,)),
-                dma((5, 2, n_z, 2)),
-                dma((2, n_dp, 2)),
+                dma((5, 2, n_z, 2, PARTS)),
+                dma((2, n_dp, 2, PARTS)),
                 dma((2 * n_vocab,)),
                 dma((2 * n_vocab,)),
                 dma((2, n_z)),

time: 74.3 us -> 60.2 us (0.81)
  Pallas kernels: 71.8 us -> 57.7 us
    pallas_call x1, Pallas kernels: 71.8 us -> 57.7 us  [body(): pl.pallas_call(functools.partial(kernel, (n_dp, n_vocab, rows, PARTS, min...]
where the time goes in v2:
time: 60.2 us; the launch traced here: 60 us
  Pallas kernels  57.7 us (96%)
  local copies, waits for them, and re-layouts  2.3 us (4%)
    pallas_call x1, Pallas kernels, body(): pl.pallas_call(functools.partial(kernel, (n_dp, n_vocab, rows, PARTS, min...  57.7 us
    unnamed x1, local copies, waits for them, and re-layouts  2.3 us

profile of v2, /device:TPU:0, one launch (start us, length us, event | category | flops | bytes accessed | tf_op | source)
XLA Modules:
  0.0 60.0 jit_solution(8604899609045804119)
XLA Ops:
  0.0 57.7 %shard_map.37 = bf16[256,2048]{1,0:T(8,128)(2,1)} custom-call(s32[2,1024]{1,0:T(2,128)} %ids_ref.1, bf16[1,128,2048]{2,1,0:T(8,128)(2,1)} %act_ref.1, bf16[512,2048]{1,0:T(8,128)(2,1)} %table_ref.1), custom_call_target="tpu_custom_call" | custom-call | tf_op jit(solution)/shard_map/pallas_call | solution.py:338
  57.7 2.3 %copy.5 = bf16[1,1,256,2048]{3,2,1,0:T(8,128)(2,1)} copy(bf16[1,1,256,2048]{3,2,1,0:T(8,128)(2,1)} %bitcast.1) | data formatting | bytes 2097152

commit v3 on v2

--- a/solution.py
+++ b/solution.py
@@ -64,16 +64,19 @@
                 greet(sec, zz * 2 + c, v)
     pl.semaphore_wait(barrier, 4 * n_vocab - 1 + 2 * (n_z - 1))
 
-    def piece(sec, dp, k, j):
-        first = pl.multiple_of(dp * rows + k * half + j * part, part)
-        return gathered.at[sec, pl.ds(first, part)]
-
-    def copy(to, sec, dp, k, j):
-        where = piece(sec, dp, k, j)
+    def piece(sec, zz, k, j, core=None):
+        core = c if core is None else core
+        first = (zz * 2 + core) * rows + k * half + (0 if j is None else j * part)
+        size = half if j is None else part
+        return gathered.at[sec, pl.ds(pl.multiple_of(first, size), size)]
+
+    def copy(to, sec, zz, k, j, core=None):
+        where = piece(sec, zz, k, j, core)
+        dp = zz * 2 + (c if core is None else core)
         return pltpu.make_async_remote_copy(
             src_ref=where, dst_ref=where,
-            send_sem=send_sem.at[lane[to], sec, dp // 2, k, j],
-            recv_sem=recv_sem.at[sec, dp, k, j],
+            send_sem=send_sem.at[lane[to], sec, zz, k],
+            recv_sem=recv_sem.at[sec, dp, k, 0 if j is None or to == "x" else j],
             device_id=targets[to], device_id_type=MESH,
         )
 
@@ -101,34 +104,43 @@
         for to in lanes:
             @pl.when(need(to, own, zz, k))
             def _():
-                copy(to, s if own else other, zz * 2 + c, k, j).start()
-
-    def arrive(sec, dp, k, j):
-        copy("sib", sec, dp, k, j).wait_recv()
-
-    def event(own, zz, k, j):
-        arrive(s if own else other, zz * 2 + c, k, j)
-        emit(own, zz, k, j, order_own if own else order_other)
-
-    def each_part(act):
-        def one(j, carry):
-            act(j)
-            return carry
-        lax.fori_loop(0, parts, one, 0)
-
-    def from_y(index):
-        near = jnp.minimum(z, n_z - 1 - z)
-        paired = index < 2 * near * parts
+                copy(to, s if own else other, zz, k, j).start()
+
+    def relay(own, zz, j):
+        sec = s if own else other
+        copy("sib", sec, zz, h, j).wait_recv()
+        emit(own, zz, h, j, order_own[:-1] if own else order_other[:-1])
+        if j == parts - 1:
+            copy("sib", sec, zz, h, None).start()
+
+    def settle(own, zz):
+        sec = s if own else other
+        copy("sib", sec, zz, 1 - h, None).wait_recv()
+        if own:
+            emit(own, zz, 1 - h, None, ("y",))
+        copy("sib", sec, zz, 1 - h, None).start()
+
+    near = jnp.minimum(z, n_z - 1 - z)
+    far_side = jnp.where(z < n_z - 1 - z, 1, -1)
+
+    def from_y(t, j):
+        index = (t - 1) * parts + j
+        delta = index // (2 * parts) + 1
         inside = index % (2 * parts)
-        delta = index // (2 * parts) + 1
-        side = 2 * (inside % 2) - 1
-        rest = index - 2 * near * parts
-        far_side = jnp.where(z < n_z - 1 - z, 1, -1)
-        zz = jnp.where(paired, z + side * delta, z + far_side * (near + 1 + rest // parts))
-        return zz, jnp.where(paired, inside // 2, rest % parts)
+        paired = delta <= near
+        zz = jnp.where(
+            paired, z + (2 * (inside % 2) - 1) * delta,
+            z + far_side * (near + 1 + index // parts - 2 * near),
+        )
+        return zz, jnp.where(paired, inside // 2, index % parts)
+
+    def y_shard(t):
+        delta = (t + 1) // 2
+        paired = z + (delta if t % 2 == 0 else -delta)
+        return jnp.where(delta <= near, paired, z + far_side * (t - near))
 
     def own_second_half(to):
-        each_part(lambda j: copy(to, s, d, 1 - h, j).start())
+        copy(to, s, z, 1 - h, None).start()
 
     def score(dp):
         tokens = gathered.at[1, pl.ds(pl.multiple_of(dp * rows, rows), rows)]
@@ -156,11 +168,9 @@
         lax.fori_loop(0, n_dp, one, 0)
 
     def sibling(sec):
-        def act(zz, carry):
+        for zz in range(n_z):
             for k in range(2):
-                each_part(lambda j: arrive(sec, zz * 2 + 1 - c, k, j))
-            return carry
-        lax.fori_loop(0, n_z, act, 0)
+                copy("sib", sec, zz, k, None, 1 - c).wait_recv()
 
     def on_both_sides(delta, act):
         for zz in (z - delta, z + delta):
@@ -169,46 +179,45 @@
                 act(zz)
 
     own_load.wait()
-    each_part(lambda j: emit(True, z, h, j, ("right", "left", "y")))
-    each_part(lambda j: emit(True, z, h, j, ("sib",)))
-    each_part(lambda j: emit(True, z, 1 - h, j, ("sib",)))
+    for j in range(parts):
+        emit(True, z, h, j, ("right", "left", "y"))
     pl.when((z > 0) & (z == n_z - 1))(lambda: own_second_half("left"))
     pl.when((z == 0) & (z < n_z - 1))(lambda: own_second_half("right"))
+    emit(True, z, h, None, ("sib",))
+    emit(True, z, 1 - h, None, ("sib",))
 
     def slot(t):
-        def links(j):
+        for j in range(parts if t < n_z else 0):
             if t + 1 < n_z:
-                on_both_sides(t + 1, lambda zz: event(True, zz, h, j))
+                on_both_sides(t + 1, lambda zz: relay(True, zz, j))
             if t == 0:
-                event(False, z, h, j)
-            elif t < n_z:
-                zz, jj = from_y((t - 1) * parts + j)
-                event(False, zz, h, jj)
-
-        if t < n_z:
-            each_part(links)
+                relay(False, z, j)
+            else:
+                zz, jj = from_y(t, j)
+                relay_y(zz, jj, j)
         if t < n_z - 1:
             pl.when((z > 0) & (t == n_z - 2 - z))(lambda: own_second_half("left"))
             pl.when((z < n_z - 1) & (t == z - 1))(lambda: own_second_half("right"))
-
-        def second(j):
-            if 1 <= t < n_z:
-                pl.when((z > 0) & (t == z))(lambda: event(True, z - 1, 1 - h, j))
-                pl.when((z < n_z - 1) & (t == n_z - 1 - z))(
-                    lambda: event(True, z + 1, 1 - h, j)
-                )
-            if t == 1:
-                event(False, z, 1 - h, j)
-            if 2 <= t < n_z:
-                on_both_sides(t, lambda zz: event(True, zz, 1 - h, j))
-            if t == n_z:
-                event(False, twin, 1 - h, j)
-            if 3 <= t:
-                zz, jj = from_y((t - 3) * parts + j)
-                pl.when(zz != twin)(lambda: event(False, zz, 1 - h, jj))
-
-        if t >= 1:
-            each_part(second)
+        if 1 <= t < n_z:
+            pl.when((z > 0) & (t == z))(lambda: settle(True, z - 1))
+            pl.when((z < n_z - 1) & (t == n_z - 1 - z))(lambda: settle(True, z + 1))
+        if t == 1:
+            settle(False, z)
+        if 2 <= t < n_z:
+            on_both_sides(t, lambda zz: settle(True, zz))
+        if t == n_z:
+            settle(False, twin)
+        if 3 <= t:
+            zz = y_shard(t - 2)
+            pl.when(zz != twin)(lambda: settle(False, zz))
+
+    def relay_y(zz, jj, j):
+        copy("sib", other, zz, h, jj).wait_recv()
+        emit(False, zz, h, jj, ("x",))
+
+        @pl.when(jj == parts - 1)
+        def _():
+            copy("sib", other, zz, h, None).start()
 
     for t in range(n_z):
         slot(t)
@@ -312,17 +321,13 @@
                 def _():
                     chain_copy(sec, zz).wait_send()
 
-    def drain(zz, carry):
-        for k in range(2):
+    for zz in range(n_z):
+        for k in (h, 1 - h):
             for own in (True, False):
                 for to in order_own if own else order_other:
                     @pl.when(need(to, own, zz, k))
                     def _():
-                        sec = s if own else other
-                        each_part(lambda j: copy(to, sec, zz * 2 + c, k, j).wait_send())
-        return carry
-
-    lax.fori_loop(0, n_z, drain, 0)
+                        copy(to, s if own else other, zz, k, None).wait_send()
 
 
 def solution(mesh):
@@ -352,7 +357,7 @@
                 pltpu.VMEM((2 * n_vocab, 2, tokens), jnp.float32),
                 pltpu.VMEM((n_z, 2, tokens), jnp.float32),
                 dma((2,)),
-                dma((5, 2, n_z, 2, PARTS)),
+                dma((5, 2, n_z, 2)),
                 dma((2, n_dp, 2, PARTS)),
                 dma((2 * n_vocab,)),
                 dma((2 * n_vocab,)),

time: 60.2 us -> 56.2 us (0.934)
  Pallas kernels: 57.7 us -> 53.7 us
    pallas_call x1, Pallas kernels: 57.7 us -> 53.7 us  [body(): pl.pallas_call(functools.partial(kernel, (n_dp, n_vocab, rows, PARTS, min...]
where the time goes in v3:
time: 56.2 us; the launch traced here: 56.1 us
  Pallas kernels  53.7 us (96%)
  local copies, waits for them, and re-layouts  2.3 us (4%)
    pallas_call x1, Pallas kernels, body(): pl.pallas_call(functools.partial(kernel, (n_dp, n_vocab, rows, PARTS, min...  53.7 us
    unnamed x1, local copies, waits for them, and re-layouts  2.3 us

profile of v3, /device:TPU:0, one launch (start us, length us, event | category | flops | bytes accessed | tf_op | source)
XLA Modules:
  0.0 56.1 jit_solution(17098763787636034029)
XLA Ops:
  0.0 53.7 %shard_map.37 = bf16[256,2048]{1,0:T(8,128)(2,1)} custom-call(s32[2,1024]{1,0:T(2,128)} %ids_ref.1, bf16[1,128,2048]{2,1,0:T(8,128)(2,1)} %act_ref.1, bf16[512,2048]{1,0:T(8,128)(2,1)} %table_ref.1), custom_call_target="tpu_custom_call" | custom-call | tf_op jit(solution)/shard_map/pallas_call | solution.py:343
  53.7 2.3 %copy.5 = bf16[1,1,256,2048]{3,2,1,0:T(8,128)(2,1)} copy(bf16[1,1,256,2048]{3,2,1,0:T(8,128)(2,1)} %bitcast.1) | data formatting | bytes 2097152

commit v4 on v3

--- a/solution.py
+++ b/solution.py
@@ -9,6 +9,7 @@
 
 MESH = pl.DeviceIdType.MESH
 PARTS = 4
+VMEM_MIB = 60
 NT = (((1,), (1,)), ((), ()))
 
 
@@ -167,10 +168,18 @@
             return carry
         lax.fori_loop(0, n_dp, one, 0)
 
+    def sibling_shard(sec, zz):
+        for k in range(2):
+            copy("sib", sec, zz, k, None, 1 - c).wait_recv()
+
     def sibling(sec):
         for zz in range(n_z):
-            for k in range(2):
-                copy("sib", sec, zz, k, None, 1 - c).wait_recv()
+            sibling_shard(sec, zz)
+
+    def early_score(zz):
+        sibling_shard(1, zz)
+        score(zz * 2)
+        score(zz * 2 + 1)
 
     def on_both_sides(delta, act):
         for zz in (z - delta, z + delta):
@@ -223,6 +232,13 @@
         slot(t)
         if t == 0:
             table_load.wait()
+        else:
+            @pl.when(s == 1)
+            def _():
+                if t == 1:
+                    early_score(z)
+                else:
+                    on_both_sides(t, early_score)
 
     def combine(load, count):
         peak = load(0)[0:1]
@@ -256,8 +272,7 @@
 
     @pl.when(s == 1)
     def _():
-        sibling(1)
-        score_all()
+        on_both_sides(1, early_score)
         group_stats[mine] = col_stats[...]
         for at in range(n_group):
             @pl.when(at != mine)
@@ -365,7 +380,7 @@
                 dma((n_z,)),
             ],
             compiler_params=pltpu.CompilerParams(
-                collective_id=0, has_side_effects=True, vmem_limit_bytes=60 * 1024 * 1024
+                collective_id=0, has_side_effects=True, vmem_limit_bytes=VMEM_MIB * 1024 * 1024
             ),
         )(token_ids, activations, embed_table)
         return grad.reshape(1, 1, half_rows, width)

time: 56.2 us -> 53.3 us (0.948)
  Pallas kernels: 53.7 us -> 50.8 us
    pallas_call x1, Pallas kernels: 53.7 us -> 50.8 us  [body(): pl.pallas_call(functools.partial(kernel, (n_dp, n_vocab, rows, PARTS, min...]
where the time goes in v4:
time: 53.3 us; the launch traced here: 53.1 us
  Pallas kernels  50.8 us (95%)
  local copies, waits for them, and re-layouts  2.3 us (4%)
    pallas_call x1, Pallas kernels, body(): pl.pallas_call(functools.partial(kernel, (n_dp, n_vocab, rows, PARTS, min...  50.8 us
    unnamed x1, local copies, waits for them, and re-layouts  2.3 us

profile of v4, /device:TPU:0, one launch (start us, length us, event | category | flops | bytes accessed | tf_op | source)
XLA Modules:
  0.0 53.1 jit_solution(10880933291573566710)
XLA Ops:
  0.0 50.8 %shard_map.37 = bf16[256,2048]{1,0:T(8,128)(2,1)} custom-call(s32[2,1024]{1,0:T(2,128)} %ids_ref.1, bf16[1,128,2048]{2,1,0:T(8,128)(2,1)} %act_ref.1, bf16[512,2048]{1,0:T(8,128)(2,1)} %table_ref.1), custom_call_target="tpu_custom_call" | custom-call | tf_op jit(solution)/shard_map/pallas_call | solution.py:358
  50.8 2.3 %copy.5 = bf16[1,1,256,2048]{3,2,1,0:T(8,128)(2,1)} copy(bf16[1,1,256,2048]{3,2,1,0:T(8,128)(2,1)} %bitcast.1) | data formatting | bytes 2097152
